TPU v7x, 32 devices: a whole 2x2x4 slice. The times are simulated.
32 devices in a mesh: fsdp: 8 (over z, y), rep: 4 (over x, core).
Axes of the slice: x: 2, y: 2, z: 4, core: 2. Of those that a mesh axis runs over, the one named last changes fastest.
Arguments:
- latents: float32 [192, 4, 1024], P(('fsdp', 'rep')), may hold values from -6 to 6
- tsteps: int32 [192], P(('fsdp', 'rep')), may hold values from 0 to 999
- labels: int32 [192], P(('fsdp', 'rep')), may hold values from 0 to 1000
- noise: float32 [192, 4, 1024], P(('fsdp', 'rep')), may hold values from -6 to 6
- layer_in: float32 [2, 384, 5376], P(None, 'fsdp'), may hold values from -0.3125 to 0.3125
- layer_out: float32 [2, 1536, 384], P(None, 'fsdp'), may hold values from -0.15625 to 0.15625
- edge_mat: float32 [384, 2457], P('fsdp'), may hold values from -4 to 4
- layer_bias: float32 [2, 5376], replicated, may hold values from -2 to 2
- top_bias: float32 [1952], replicated, may hold values from -2 to 2
- in_rows: float32 [2, 384], P(None, 'fsdp'), may hold values from 0.0005 to 0.2
- in_cols: float32 [2, 5376], replicated, may hold values from 0.005 to 0.05
- out_rows: float32 [2, 1536], P(None, 'fsdp'), may hold values from 0.0005 to 0.2
- out_cols: float32 [2, 384], replicated, may hold values from 0.005 to 0.05
- edge_rows: float32 [384], P('fsdp'), may hold values from 0.0005 to 0.2
- edge_cols: float32 [2457], replicated, may hold values from 0.005 to 0.05
- layer_bias_v: float32 [2, 5376], replicated, may hold values from 0.005 to 0.05
- top_bias_v: float32 [1952], replicated, may hold values from 0.005 to 0.05
Outputs:
- loss: float32 [], replicated
- layer_in_new: float32 [2, 384, 5376], P(None, 'fsdp')
- layer_out_new: float32 [2, 1536, 384], P(None, 'fsdp')
- edge_mat_new: float32 [384, 2457], P('fsdp')
- layer_bias_new: float32 [2, 5376], replicated
- top_bias_new: float32 [1952], replicated
- in_rows_new: float32 [2, 384], P(None, 'fsdp')
- in_cols_new: float32 [2, 5376], replicated
- out_rows_new: float32 [2, 1536], P(None, 'fsdp')
- out_cols_new: float32 [2, 384], replicated
- edge_rows_new: float32 [384], P('fsdp')
- edge_cols_new: float32 [2457], replicated
- layer_bias_v_new: float32 [2, 5376], replicated
- top_bias_v_new: float32 [1952], replicated
- clip_roots: float32 [5], replicated
All inputs are finite; a program needn't handle non-finite values.
Results may differ from a plain program's by a relative error of at most 0.0015.
The roundings to bfloat16 on the way count: a program that leaves them out, or rounds other values in their place, can miss the bound.
Values may be sent and summed in bfloat16 or wider, within the bound.
A program may use at most 256 MiB of HBM per device.

v0:
```python
import math
import jax
import jax.numpy as jnp
from jax import lax
from jax.sharding import PartitionSpec as P

D = 384
HEADS = 6
HEAD_DIM = 64
FF = 1536
CHANNELS = 4
PATCH = 2
GRID = 32
TSTEPS = 1000
NCLS = 1001
FREQ = 256
MICRO = 3
PATCH_IN = 16
eps_norm = 1e-06
eps_stat = 1e-30
decay = 0.5
rate = 0.01
clip_level = 1.0


def round_value(values):
    return lax.optimization_barrier(values.astype(jnp.bfloat16)).astype(jnp.float32)


def rounders():
    rounding = jax.custom_vjp(round_value)

    def keep_forward(values):
        return (round_value(values), None)

    def pass_backward(kept, grad):
        return (grad,)

    rounding.defvjp(keep_forward, pass_backward)

    def unchanged(values):
        return values

    backing = jax.custom_vjp(unchanged)

    def back_forward(values):
        return (values, None)

    def back_backward(kept, grad):
        return (round_value(grad),)

    backing.defvjp(back_forward, back_backward)
    return (rounding, backing)


def low(values):
    return rounders()[0](values)


def low_back(values):
    return rounders()[1](values)


def mult(left, right, form):
    return jnp.einsum(form, left, right, preferred_element_type=jnp.float32)


def normalize(values):
    center = values - jnp.mean(values, axis=-1, keepdims=True)
    spread = jnp.mean(center * center, axis=-1, keepdims=True)
    return center * lax.rsqrt(spread + eps_norm)


def mix_weights(tsteps):
    betas = 0.0001 + (0.02 - 0.0001) * jnp.arange(TSTEPS, dtype=jnp.float32) / (TSTEPS - 1)
    alpha_bar = jnp.exp(jnp.cumsum(jnp.log(1.0 - betas)))
    picked = jnp.arange(TSTEPS)[None, :] == tsteps[:, None]
    return jnp.sum(jnp.where(picked, alpha_bar[None, :], 0.0), axis=1)


def patchify(latent_rows):
    images = latent_rows.shape[0]
    grid_side = GRID // PATCH
    shaped = latent_rows.reshape(images, CHANNELS, grid_side, PATCH, grid_side, PATCH)
    shaped = jnp.transpose(shaped, (0, 2, 4, 1, 3, 5))
    return shaped.reshape(images, grid_side * grid_side, CHANNELS * PATCH * PATCH)


def position_table():
    grid_side = GRID // PATCH
    quarter = D // 4
    omegas = 1.0 / 10000.0 ** (jnp.arange(quarter, dtype=jnp.float32) / quarter)
    places = jnp.arange(grid_side * grid_side)
    across = (places % grid_side).astype(jnp.float32)
    downward = (places // grid_side).astype(jnp.float32)

    def one_axis(coords):
        angles = coords[:, None] * omegas[None, :]
        return jnp.concatenate([jnp.sin(angles), jnp.cos(angles)], axis=1)

    return jnp.concatenate([one_axis(across), one_axis(downward)], axis=1)


def time_features(tsteps):
    half_freq = FREQ // 2
    frequencies = jnp.exp(-math.log(10000.0) * jnp.arange(half_freq, dtype=jnp.float32) / half_freq)
    angles = tsteps.astype(jnp.float32)[:, None] * frequencies[None, :]
    return jnp.concatenate([jnp.cos(angles), jnp.sin(angles)], axis=1)


def block(tokens, condition, weights, weights_down, biases):
    images = tokens.shape[0]
    tok_count = tokens.shape[1]
    modulation = low_back(mult(condition, weights[:, : 6 * D], "bd,de->be") + biases[: 6 * D])
    shift_attn = modulation[:, 0:D][:, None]
    scale_attn = modulation[:, D : 2 * D][:, None]
    gate_attn = modulation[:, 2 * D : 3 * D][:, None]
    shift_mlp = modulation[:, 3 * D : 4 * D][:, None]
    scale_mlp = modulation[:, 4 * D : 5 * D][:, None]
    gate_mlp = modulation[:, 5 * D : 6 * D][:, None]
    normed = low(normalize(tokens) * (1.0 + scale_attn) + shift_attn)
    bias_qkv = jnp.concatenate(
        [biases[6 * D : 7 * D], jnp.zeros_like(biases[:D]), biases[7 * D : 8 * D]]
    )
    project = low(low_back(mult(normed, weights[:, 6 * D : 9 * D], "btd,de->bte") + bias_qkv))
    queries = project[..., :D].reshape(images, tok_count, HEADS, HEAD_DIM)
    keys_all = project[..., D : 2 * D].reshape(images, tok_count, HEADS, HEAD_DIM)
    values_all = project[..., 2 * D :].reshape(images, tok_count, HEADS, HEAD_DIM)
    scores = low_back(mult(queries, keys_all, "bqhe,bkhe->bhqk") * HEAD_DIM ** (-0.5))
    weights_soft = low(jax.nn.softmax(scores, axis=-1))
    attended = low(low_back(mult(weights_soft, values_all, "bhqk,bkhe->bqhe"))).reshape(
        images, tok_count, D
    )
    branch = low_back(
        mult(attended, weights[:, 9 * D : 10 * D], "btd,de->bte") + biases[8 * D : 9 * D]
    )
    tokens = tokens + gate_attn * branch
    normed_mlp = low(normalize(tokens) * (1.0 + scale_mlp) + shift_mlp)
    inner = low_back(
        mult(normed_mlp, weights[:, 10 * D :], "btd,df->btf") + biases[9 * D : 9 * D + FF]
    )
    activated = low(jax.nn.gelu(inner, approximate=True))
    outward = low_back(mult(activated, weights_down, "btf,fd->btd") + biases[9 * D + FF :])
    return tokens + gate_mlp * outward


def image_loss(params, latents, tsteps, labels, noise):
    layer_in, layer_out, edge_mat, layer_bias, top_bias = params
    depth = layer_in.shape[0]
    alphas = mix_weights(tsteps)
    noisy = (
        jnp.sqrt(alphas)[:, None, None] * latents + jnp.sqrt(1.0 - alphas)[:, None, None] * noise
    )
    patches = low(patchify(noisy))
    target = patchify(noise)
    edge_low = low(edge_mat)
    start_freq = NCLS + PATCH_IN
    start_tail = start_freq + FREQ
    class_cols = edge_low[:, :NCLS]
    patch_cols = edge_low[:, NCLS:start_freq]
    freq_cols = edge_low[:, start_freq:start_tail]
    time_second = edge_low[:, start_tail : start_tail + D]
    final_cols = edge_low[:, start_tail + D : start_tail + 3 * D]
    head_cols = edge_low[:, start_tail + 3 * D :]
    tokens = (
        low_back(mult(patches, patch_cols, "btp,dp->btd") + top_bias[:D]) + position_table()[None]
    )
    features = low(time_features(tsteps))
    time_first = low_back(mult(features, freq_cols, "bf,df->bd") + top_bias[D : 2 * D])
    time_out = low_back(
        mult(low(jax.nn.silu(time_first)), time_second, "bd,de->be") + top_bias[2 * D : 3 * D]
    )
    class_emb = jnp.take(class_cols, labels, axis=1).T
    condition = low(jax.nn.silu(time_out + class_emb))
    for layer_index in range(depth):
        tokens = block(
            tokens,
            condition,
            low(layer_in[layer_index]),
            low(layer_out[layer_index]),
            layer_bias[layer_index],
        )
    closing = low_back(mult(condition, final_cols, "bd,de->be") + top_bias[3 * D : 5 * D])
    normed = low(normalize(tokens) * (1.0 + closing[:, None, D:]) + closing[:, None, :D])
    predicted = low_back(mult(normed, head_cols, "btd,dp->btp") + top_bias[5 * D :])
    misfit = predicted[..., :PATCH_IN] - target
    return jnp.sum(misfit * misfit)


def fetch_weights(layer_in, layer_out, edge_mat, again):
    gathered_in = []
    gathered_out = []
    for layer_index in range(layer_in.shape[0]):
        own_in = layer_in[layer_index].astype(jnp.bfloat16)
        own_out = layer_out[layer_index].astype(jnp.bfloat16)
        if again:
            full_in, full_out = (
                lax.all_gather(own_in, "fsdp", axis=0, tiled=True),
                lax.all_gather(own_out, "fsdp", axis=0, tiled=True),
            )
        else:
            full_in, full_out = (
                lax.all_gather(own_in, "fsdp", axis=0, tiled=True),
                lax.all_gather(own_out, "fsdp", axis=0, tiled=True),
            )
        gathered_in.append(full_in)
        gathered_out.append(full_out)
    if again:
        full_edge = lax.all_gather(edge_mat.astype(jnp.bfloat16), "fsdp", axis=0, tiled=True)
    else:
        full_edge = lax.all_gather(edge_mat.astype(jnp.bfloat16), "fsdp", axis=0, tiled=True)
    return (
        jnp.stack(gathered_in).astype(jnp.float32),
        jnp.stack(gathered_out).astype(jnp.float32),
        full_edge.astype(jnp.float32),
    )


def step_of(grad, rows_new, cols_new, rows_mean):
    second = rows_new[:, :, None] * cols_new[:, None, :] / rows_mean[:, None, None]
    return grad * lax.rsqrt(second)


def plain(weight, grad, moment):
    moment_new = decay * moment + (1.0 - decay) * (grad * grad + eps_stat)
    update = grad * lax.rsqrt(moment_new)
    root = jnp.sqrt(jnp.mean(update * update, axis=-1, keepdims=True))
    return (weight - rate * update / jnp.maximum(1.0, root / clip_level), moment_new)


def shards(
    latents,
    tsteps,
    labels,
    noise,
    layer_in,
    layer_out,
    edge_mat,
    layer_bias,
    top_bias,
    in_rows,
    in_cols,
    out_rows,
    out_cols,
    edge_rows,
    edge_cols,
    layer_bias_v,
    top_bias_v,
):
    per_micro = latents.shape[0] // MICRO
    loss_sum = jnp.zeros((), jnp.float32)
    gradients = None

    def add_grads(total_grads, grads_now):
        if total_grads is None:
            return grads_now
        return jax.tree.map(jnp.add, total_grads, grads_now)

    for micro_index in range(MICRO):
        start = micro_index * per_micro
        data_now = (
            latents[start : start + per_micro],
            tsteps[start : start + per_micro],
            labels[start : start + per_micro],
            noise[start : start + per_micro],
        )
        full_in, full_out, full_edge = fetch_weights(layer_in, layer_out, edge_mat, False)
        loss_part = image_loss((full_in, full_out, full_edge, layer_bias, top_bias), *data_now)
        loss_sum = loss_sum + loss_part
        again_in, again_out, again_edge = fetch_weights(layer_in, layer_out, edge_mat, True)
        params = (again_in, again_out, again_edge, layer_bias, top_bias)
        recomputed, pullback = jax.vjp(lambda params_now: image_loss(params_now, *data_now), params)
        (grads_now,) = pullback(jnp.ones_like(recomputed))
        gradients = add_grads(gradients, grads_now)
    grad_in_full, grad_out_full, grad_edge_full, grad_lbias, grad_tbias = gradients
    shard_in, shard_out, shard_edge = (
        lax.psum_scatter(grad_in_full, "fsdp", scatter_dimension=1, tiled=True),
        lax.psum_scatter(grad_out_full, "fsdp", scatter_dimension=1, tiled=True),
        lax.psum_scatter(grad_edge_full[None], "fsdp", scatter_dimension=1, tiled=True),
    )
    shard_in, shard_out, shard_edge = lax.psum((shard_in, shard_out, shard_edge), "rep")
    bias_in_sum, bias_top_sum, loss_total = lax.psum(
        (grad_lbias, grad_tbias, loss_sum), ("fsdp", "rep")
    )
    fsdp_count = lax.axis_size("fsdp")
    tok_total = latents.shape[0] * fsdp_count * lax.axis_size("rep") * (GRID // PATCH) ** 2
    scale_grad = 1.0 / (PATCH_IN * math.sqrt(tok_total))
    loss = loss_total / (tok_total * PATCH_IN)
    grad_in = shard_in * scale_grad
    grad_out = shard_out * scale_grad
    grad_edge = shard_edge * scale_grad
    full_rows_in = layer_in.shape[1] * fsdp_count
    full_rows_out = layer_out.shape[1] * fsdp_count
    full_rows_edge = edge_mat.shape[0] * fsdp_count
    square_in = grad_in * grad_in + eps_stat
    square_out = grad_out * grad_out + eps_stat
    square_edge = grad_edge * grad_edge + eps_stat
    rows_in_new = decay * in_rows + (1.0 - decay) * jnp.mean(square_in, axis=2)
    rows_out_new = decay * out_rows + (1.0 - decay) * jnp.mean(square_out, axis=2)
    rows_edge_new = decay * edge_rows[None] + (1.0 - decay) * jnp.mean(square_edge, axis=2)
    col_in, total_in, col_out, total_out, col_edge, total_edge = lax.psum(
        (
            jnp.sum(square_in, axis=1),
            jnp.sum(rows_in_new, axis=1),
            jnp.sum(square_out, axis=1),
            jnp.sum(rows_out_new, axis=1),
            jnp.sum(square_edge, axis=1),
            jnp.sum(rows_edge_new, axis=1),
        ),
        "fsdp",
    )
    cols_in_new = decay * in_cols + (1.0 - decay) * col_in / full_rows_in
    cols_out_new = decay * out_cols + (1.0 - decay) * col_out / full_rows_out
    cols_edge_new = decay * edge_cols[None] + (1.0 - decay) * col_edge / full_rows_edge
    update_in = step_of(grad_in, rows_in_new, cols_in_new, total_in / full_rows_in)
    update_out = step_of(grad_out, rows_out_new, cols_out_new, total_out / full_rows_out)
    update_edge = step_of(grad_edge, rows_edge_new, cols_edge_new, total_edge / full_rows_edge)
    sum_in, sum_out, sum_edge = lax.psum(
        (
            jnp.sum(update_in * update_in, axis=(1, 2)),
            jnp.sum(update_out * update_out, axis=(1, 2)),
            jnp.sum(update_edge * update_edge, axis=(1, 2)),
        ),
        "fsdp",
    )
    mean_sq_in = sum_in / (full_rows_in * grad_in.shape[2])
    mean_sq_out = sum_out / (full_rows_out * grad_out.shape[2])
    mean_sq_edge = sum_edge / (full_rows_edge * grad_edge.shape[2])
    roots_in = jnp.sqrt(mean_sq_in)
    roots_out = jnp.sqrt(mean_sq_out)
    roots_edge = jnp.sqrt(mean_sq_edge)
    factor_in = jnp.maximum(1.0, roots_in / clip_level)[:, None, None]
    factor_out = jnp.maximum(1.0, roots_out / clip_level)[:, None, None]
    factor_edge = jnp.maximum(1.0, roots_edge / clip_level)[:, None, None]
    in_new = layer_in - rate * update_in / factor_in
    out_new = layer_out - rate * update_out / factor_out
    edge_new = (edge_mat[None] - rate * update_edge / factor_edge)[0]
    clip_roots = jnp.concatenate([roots_in, roots_out, roots_edge])
    lbias_new, lbias_v_new = plain(layer_bias, bias_in_sum * scale_grad, layer_bias_v)
    tbias_new, tbias_v_new = plain(top_bias, bias_top_sum * scale_grad, top_bias_v)
    return (
        loss,
        in_new,
        out_new,
        edge_new,
        lbias_new,
        tbias_new,
        rows_in_new,
        cols_in_new,
        rows_out_new,
        cols_out_new,
        rows_edge_new[0],
        cols_edge_new[0],
        lbias_v_new,
        tbias_v_new,
        clip_roots,
    )


def solution(mesh):
    placed = (
        P(("fsdp", "rep"), None, None),
        P(("fsdp", "rep")),
        P(("fsdp", "rep")),
        P(("fsdp", "rep"), None, None),
        P(None, "fsdp", None),
        P(None, "fsdp", None),
        P("fsdp", None),
        P(),
        P(),
        P(None, "fsdp"),
        P(),
        P(None, "fsdp"),
        P(),
        P("fsdp"),
        P(),
        P(),
        P(),
    )
    return jax.shard_map(
        shards,
        mesh=mesh,
        in_specs=placed,
        out_specs=(
            P(),
            P(None, "fsdp", None),
            P(None, "fsdp", None),
            P("fsdp", None),
            P(),
            P(),
            P(None, "fsdp"),
            P(),
            P(None, "fsdp"),
            P(),
            P("fsdp"),
            P(),
            P(),
            P(),
            P(),
        ),
        check_vma=False,
    )
```

profile of v0, /device:TPU:0, one launch (start us, length us, event | category | flops | bytes accessed | tf_op | source)
XLA Modules:
  0.0 1379.7 jit_solution(4260965202607381053)
XLA Ops:
  37.3 16.8 %all-gather.18.cloned.1.call-done = bf16[1,1536,384]{2,1,0:T(8,128)(2,1)} async-done(((bf16[1,192,384]{2,1,0:T(8,128)(2,1)}), bf16[1,1536,384]{2,1,0:T(8,128)(2,1)}) %all-gather.18.cloned.1.call-update) | async-done | bytes 1179664 | tf_op jit(solution)/shard_map/all_gather | solution.py:204
  54.1 42.0 %all-gather.14.cloned.1.call-done = bf16[1,1536,384]{2,1,0:T(8,128)(2,1)} async-done(((bf16[1,192,384]{2,1,0:T(8,128)(2,1)}), bf16[1,1536,384]{2,1,0:T(8,128)(2,1)}) %all-gather.14.cloned.1.call-update) | async-done | bytes 1179664 | tf_op jit(solution)/shard_map/all_gather | solution.py:204
  96.1 48.7 %all-gather.10.cloned.1.call-done = bf16[384,2457]{1,0:T(8,128)(2,1)} async-done(((bf16[48,2457]{1,0:T(8,128)(2,1)}), bf16[384,2457]{1,0:T(8,128)(2,1)}) %all-gather.10.cloned.1.call-update) | async-done | bytes 1886992 | tf_op jit(solution)/shard_map/all_gather | solution.py:211
  166.5 51.5 %all-gather.12.cloned.1.call-done = bf16[1,384,5376]{2,1,0:T(8,128)(2,1)} async-done(((bf16[1,48,5376]{2,1,0:T(8,128)(2,1)}), bf16[1,384,5376]{2,1,0:T(8,128)(2,1)}) %all-gather.12.cloned.1.call-update) | async-done | bytes 4128784 | tf_op jit(solution)/shard_map/all_gather | solution.py:203
  223.5 67.7 %all-gather.16.cloned.1.call-done = bf16[1,384,5376]{2,1,0:T(8,128)(2,1)} async-done(((bf16[1,48,5376]{2,1,0:T(8,128)(2,1)}), bf16[1,384,5376]{2,1,0:T(8,128)(2,1)}) %all-gather.16.cloned.1.call-update) | async-done | bytes 4128784 | tf_op jit(solution)/shard_map/all_gather | solution.py:203
  340.5 4.7 multiply_convert_fusion.9
  355.5 4.9 fusion.389
  367.2 3.2 multiply_convert_fusion.8
  376.0 4.6 multiply_convert_fusion.7
  389.3 4.7 fusion.386
  402.6 5.0 multiply_convert_fusion.11
  417.7 4.7 fusion.392
  429.2 3.2 multiply_convert_fusion.10
  435.2 3.2 multiply_convert_fusion.6
  467.6 3.1 fusion.162
  521.7 3.7 multiply_reduce_fusion.35
  551.9 3.0 fusion.150
  592.4 3.0 fusion.170
  687.2 6.5 add_bitcast_fusion.6
  693.7 9.1 copy.871
  761.3 3.3 add_bitcast_fusion.2
  764.7 5.1 add_bitcast_fusion
  769.8 12.6 add_bitcast_fusion.4
  782.4 11.1 add_bitcast_fusion.1
  793.5 20.9 %add_add_fusion = f32[2,384,5376]{2,1,0:T(8,128)} fusion(f32[1,384,5376]{2,1,0:T(8,128)} %add_bitcast_fusion, f32[1,384,5376]{2,1,0:T(8,128)} %get-tuple-element.452, f32[1,384,5376]{2,1,0:T(8,128)S(1)} %add_bitcast_fusion.2, f32[1,384,5376]{2,1,0:T(8,128)} %get-tuple-element.453, f32[1,384,5376]{2,1,0:T(8,128)} %get-tuple-element.454, ...), kind=kLoop, calls=%fused_computation.15 | loop fusion | flops 20643840 | bytes 66060288 | tf_op jit(solution)/shard_map/add | solution.py:257
  830.7 40.9 %all-reduce.176 = (f32[]{:T(128)}, f32[2,5376]{1,0:T(2,128)S(1)}, f32[1952]{0:T(1024)S(1)}) all-reduce(f32[]{:T(128)S(6)} %add.2146, f32[2,5376]{1,0:T(2,128)S(1)} %add_add_fusion.26, f32[1952]{0:T(1024)S(1)} %add_add_fusion.27), channel_id=1, replica_groups=mesh['fsdp'=8,'rep'=4] {'fsdp','rep'}, use_global_device_ids=true, to_apply=%region_50.52 | all-reduce | flops 12705 | bytes 101640 | tf_op jit(solution)/shard_map/psum | solution.py:282
  876.3 73.4 %reduce-scatter.5.cloned.1.call-done = f32[2,192,384]{2,1,0:T(8,128)} async-done(((f32[2,1536,384]{2,1,0:T(8,128)}), f32[2,192,384]{2,1,0:T(8,128)}) %reduce-scatter.5.cloned.1.call-update) | async-done | bytes 589840 | tf_op jit(solution)/shard_map/reduce_scatter | solution.py:278
  949.7 279.4 %reduce-scatter.3.cloned.1.call-done = f32[2,48,5376]{2,1,0:T(8,128)} async-done(((f32[2,384,5376]{2,1,0:T(8,128)}), f32[2,48,5376]{2,1,0:T(8,128)}) %reduce-scatter.3.cloned.1.call-update) | async-done | bytes 2064400 | tf_op jit(solution)/shard_map/reduce_scatter | solution.py:277
  1229.9 69.9 %all-reduce.185.cloned.1.call-done = (f32[2,48,5376]{2,1,0:T(8,128)}, f32[2,192,384]{2,1,0:T(8,128)}, f32[1,48,2457]{2,1,0:T(8,128)}) async-done(((f32[2,48,5376]{2,1,0:T(8,128)}, f32[2,192,384]{2,1,0:T(8,128)}, f32[1,48,2457]{2,1,0:T(8,128)}), (f32[2,48,5376]{2,1,0:T(8,128)}, f32[2,192,384]{2,1,0:T(8,128)}, f32[1,48,2457]{2,1,0:T(8,128)})) %all-reduce.185.cloned.1.call-update) | async-done | bytes 3125968 | tf_op jit(solution)/shard_map/psum | solution.py:281
  1305.7 37.6 %all-reduce.178 = (f32[2]{0:T(128)S(1)}, f32[2,5376]{1,0:T(2,128)S(1)}, f32[2]{0:T(128)S(1)}, f32[2,384]{1,0:T(2,128)S(1)}, f32[1]{0:T(128)}, /*index=5*/f32[1,2457]{1,0:T(1,128)S(1)}) all-reduce(f32[2]{0:T(128)S(1)} %get-tuple-element.165, f32[2,5376]{1,0:T(2,128)S(1)} %get-tuple-element.73, ...), channel_id=1, replica_groups=mesh['fsdp'=8,'rep'=4] {'fsdp'}, use_global_device_ids=true, to_apply=%region_159.162 | all-reduce | flops 13982 | bytes 111856 | tf_op jit(solution)/shard_map/psum | solution.py:301
  1346.0 17.8 %all-reduce.177 = (f32[2]{0:T(128)S(1)}, f32[2]{0:T(128)S(1)}, f32[1]{0:T(128)}) all-reduce(f32[2]{0:T(128)S(1)} %multiply_reduce_fusion.12, f32[2]{0:T(128)S(1)} %multiply_reduce_fusion.70, f32[1]{0:T(128)} %bitcast.206), channel_id=1, replica_groups=mesh['fsdp'=8,'rep'=4] {'fsdp'}, use_global_device_ids=true, to_apply=%region_161.164 | all-reduce | flops 5 | bytes 40 | tf_op jit(solution)/shard_map/psum | solution.py:318
  1366.5 3.6 divide_subtract_fusion
  (1759 shorter events, 483.3 us)
Async XLA Ops:
  7.2 46.9 %all-gather.18.cloned.1.call-start = ((), (), s32[]{:S(2)}) async-start(), calls=%async_computation.8 | async-start | bytes 1327104 | tf_op jit(solution)/shard_map/all_gather | solution.py:204
  9.3 86.8 %all-gather.14.cloned.1.call-start = ((), (), s32[]{:S(2)}) async-start(), calls=%async_computation.6 | async-start | bytes 1327104 | tf_op jit(solution)/shard_map/all_gather | solution.py:204
  10.0 134.7 %all-gather.10.cloned.1.call-start = ((), (), s32[]{:S(2)}) async-start(), calls=%async_computation.2 | async-start | bytes 2211840 | tf_op jit(solution)/shard_map/all_gather | solution.py:211
  11.9 206.1 %all-gather.12.cloned.1.call-start = ((), (), s32[]{:S(2)}) async-start(), calls=%async_computation.5 | async-start | bytes 4644864 | tf_op jit(solution)/shard_map/all_gather | solution.py:203
  13.1 278.0 %all-gather.16.cloned.1.call-start = ((), (), s32[]{:S(2)}) async-start(), calls=%async_computation.7 | async-start | bytes 4644864 | tf_op jit(solution)/shard_map/all_gather | solution.py:203
  13.7 860.6 %all-reduce.183.cloned.1.call-start = ((), (), s32[]{:S(2)}) async-start(), calls=%async_computation.9 | async-start | bytes 7864320
  17.3 132.3 %copy-start.553 = (bf16[2,256]{1,0:T(2,128)(2,1)}, bf16[2,256]{1,0:T(2,128)(2,1)S(1)}, u32[]{:S(2)}) copy-start(bf16[2,256]{1,0:T(2,128)(2,1)S(1)} %pad_maximum_fusion.3) | copy-start | bytes 3076
  17.3 128.6 %copy-start.555 = (bf16[2,256]{1,0:T(2,128)(2,1)}, bf16[2,256]{1,0:T(2,128)(2,1)S(1)}, u32[]{:S(2)}) copy-start(bf16[2,256]{1,0:T(2,128)(2,1)S(1)} %pad_maximum_fusion.4) | copy-start | bytes 3076
  17.3 130.4 %copy-start.557 = (bf16[2,256]{1,0:T(2,128)(2,1)}, bf16[2,256]{1,0:T(2,128)(2,1)S(1)}, u32[]{:S(2)}) copy-start(bf16[2,256]{1,0:T(2,128)(2,1)S(1)} %pad_maximum_fusion.5) | copy-start | bytes 3076
  160.5 140.3 %copy-start.12 = (f32[2,256,384]{2,1,0:T(8,128)}, f32[2,256,384]{2,1,0:T(8,128)S(1)}, u32[]{:S(2)}) copy-start(f32[2,256,384]{2,1,0:T(8,128)S(1)} %get-tuple-element.368) | copy-start | bytes 2359300
  160.5 140.3 %copy-start.326 = (f32[2,256]{1,0:T(2,128)}, f32[2,256]{1,0:T(2,128)S(1)}, u32[]{:S(2)}) copy-start(f32[2,256]{1,0:T(2,128)S(1)} %broadcast_multiply_fusion.10) | copy-start | bytes 6148
  162.0 138.6 %copy-start.15 = (f32[2,256,384]{2,1,0:T(8,128)}, f32[2,256,384]{2,1,0:T(8,128)S(1)}, u32[]{:S(2)}) copy-start(f32[2,256,384]{2,1,0:T(8,128)S(1)} %get-tuple-element.351) | copy-start | bytes 2359300
  162.0 138.6 %copy-start.328 = (f32[2,256]{1,0:T(2,128)}, f32[2,256]{1,0:T(2,128)S(1)}, u32[]{:S(2)}) copy-start(f32[2,256]{1,0:T(2,128)S(1)} %broadcast_multiply_fusion.5) | copy-start | bytes 6148
  162.8 137.5 %copy-start.9 = (f32[2,256,384]{2,1,0:T(8,128)}, f32[2,256,384]{2,1,0:T(8,128)S(1)}, u32[]{:S(2)}) copy-start(f32[2,256,384]{2,1,0:T(8,128)S(1)} %get-tuple-element.385) | copy-start | bytes 2359300
  162.8 137.5 %copy-start.324 = (f32[2,256]{1,0:T(2,128)}, f32[2,256]{1,0:T(2,128)S(1)}, u32[]{:S(2)}) copy-start(f32[2,256]{1,0:T(2,128)S(1)} %broadcast_multiply_fusion.15) | copy-start | bytes 6148
  163.1 137.8 %copy-start.425 = (f32[2,256]{1,0:T(2,128)}, f32[2,256]{1,0:T(2,128)S(1)}, u32[]{:S(2)}) copy-start(f32[2,256]{1,0:T(2,128)S(1)} %fusion.287) | copy-start | bytes 6148
  163.6 137.0 %copy-start.427 = (f32[2,256]{1,0:T(2,128)}, f32[2,256]{1,0:T(2,128)S(1)}, u32[]{:S(2)}) copy-start(f32[2,256]{1,0:T(2,128)S(1)} %fusion.292) | copy-start | bytes 6148
  163.6 136.7 %copy-start.423 = (f32[2,256]{1,0:T(2,128)}, f32[2,256]{1,0:T(2,128)S(1)}, u32[]{:S(2)}) copy-start(f32[2,256]{1,0:T(2,128)S(1)} %fusion.282) | copy-start | bytes 6148
  165.9 125.2 %copy-start.297 = (bf16[2,384]{1,0:T(2,128)(2,1)S(1)}, bf16[2,384]{1,0:T(2,128)(2,1)}, u32[]{:S(2)}) copy-start(bf16[2,384]{1,0:T(2,128)(2,1)} %copy-done.296) | copy-start | bytes 4612
  219.8 73.2 %copy-start.301 = (bf16[2,384]{1,0:T(2,128)(2,1)S(1)}, bf16[2,384]{1,0:T(2,128)(2,1)}, u32[]{:S(2)}) copy-start(bf16[2,384]{1,0:T(2,128)(2,1)} %copy-done.300) | copy-start | bytes 4612
  702.9 246.8 %reduce-scatter.5.cloned.1.call-start = ((), (), s32[]{:S(2)}) async-start(), calls=%async_computation.4 | async-start | bytes 5308416 | tf_op jit(solution)/shard_map/reduce_scatter | solution.py:278
  729.1 500.0 %reduce-scatter.3.cloned.1.call-start = ((), (), s32[]{:S(2)}) async-start(), calls=%async_computation.3 | async-start | bytes 18579456 | tf_op jit(solution)/shard_map/reduce_scatter | solution.py:277
  814.5 485.4 %all-reduce.185.cloned.1.call-start = ((), (), s32[]{:S(2)}) async-start(), calls=%async_computation.10 | async-start | bytes 6291456 | tf_op jit(solution)/shard_map/psum | solution.py:281
  829.7 399.5 %copy-start.263 = (f32[2,5376]{1,0:T(2,128)S(1)}, f32[2,5376]{1,0:T(2,128)}, u32[]{:S(2)}) copy-start(f32[2,5376]{1,0:T(2,128)} %param.28) | copy-start | bytes 129028
  872.2 430.3 %copy-start.422 = (f32[1952]{0:T(1024)}, f32[1952]{0:T(1024)S(1)}, u32[]{:S(2)}) copy-start(f32[1952]{0:T(1024)S(1)} %get-tuple-element.158) | copy-start | bytes 23428
  874.3 428.2 %copy-start.264 = (f32[2,5376]{1,0:T(2,128)}, f32[2,5376]{1,0:T(2,128)S(1)}, u32[]{:S(2)}) copy-start(f32[2,5376]{1,0:T(2,128)S(1)} %get-tuple-element.160) | copy-start | bytes 129028
  1229.1 75.7 %copy-start.572 = (f32[2,192]{1,0:T(2,128)S(1)}, f32[2,192]{1,0:T(2,128)}, u32[]{:S(2)}) copy-start(f32[2,192]{1,0:T(2,128)} %param.32) | copy-start | bytes 4612
  1229.1 75.9 %copy-start.578 = (f32[48]{0:T(128)S(1)}, f32[48]{0:T(128)}, u32[]{:S(2)}) copy-start(f32[48]{0:T(128)} %param.34) | copy-start | bytes 580
  1229.1 76.5 %copy-start.576 = (f32[2,48]{1,0:T(2,128)S(1)}, f32[2,48]{1,0:T(2,128)}, u32[]{:S(2)}) copy-start(f32[2,48]{1,0:T(2,128)} %param.30) | copy-start | bytes 1156
  1229.1 114.9 %copy-start.342 = (f32[2457]{0:T(1024)S(1)}, f32[2457]{0:T(1024)}, u32[]{:S(2)}) copy-start(f32[2457]{0:T(1024)} %broadcast_multiply_fusion) | copy-start | bytes 29488
  1229.2 114.9 %copy-start.559 = (f32[2,384]{1,0:T(2,128)S(1)}, f32[2,384]{1,0:T(2,128)}, u32[]{:S(2)}) copy-start(f32[2,384]{1,0:T(2,128)} %param.33) | copy-start | bytes 9220
  1229.2 115.0 %copy-start.388 = (f32[2,5376]{1,0:T(2,128)S(1)}, f32[2,5376]{1,0:T(2,128)}, u32[]{:S(2)}) copy-start(f32[2,5376]{1,0:T(2,128)} %param.31) | copy-start | bytes 129028
  (573 other events, 2656.7 us)
Sparse Core Ops, SparseCore 0:
  10.2 43.8 all-gather.17
  56.2 39.7 all-gather.13
  98.3 46.4 all-gather.9
  147.4 70.5 all-gather.11
  220.6 70.4 all-gather.15
  703.0 148.1 all-reduce.182
  854.9 94.8 reduce-scatter.4
  953.7 275.4 reduce-scatter.2
  1232.2 67.5 all-reduce.184
where the time goes:
time: 1390 us; the launch traced here: 1380 us
  waiting for transfers between devices  651 us (47%)
  matrix products  306 us (22%)
  other arithmetic  171 us (12%)
  local copies, waits for them, and re-layouts  128 us (9%)
  blocking collectives  96.2 us (7%)
  between operations  27.5 us (2%)
    dot_general x159, matrix products, mult(): return jnp.einsum(form, left, right, preferred_element_type=jnp.float32)  285 us
    reduce_scatter x1, waiting for transfers between devices, shards(): lax.psum_scatter(grad_in_full, 'fsdp', scatter_dimension=1, tiled=True)  279 us
    all_gather x2, waiting for transfers between devices, fetch_weights(): lax.all_gather(own_in, 'fsdp', axis=0, tiled=True)  119 us
    reduce_scatter x1, waiting for transfers between devices, shards(): lax.psum_scatter(grad_out_full, 'fsdp', scatter_dimension=1, tiled=True)  73.4 us
    psum x1, waiting for transfers between devices, shards(): lax.psum((shard_in, shard_out, shard_edge), 'rep')  69.9 us
    all_gather x2, waiting for transfers between devices, fetch_weights(): lax.all_gather(own_out, 'fsdp', axis=0, tiled=True)  58.8 us
    all_gather x1, waiting for transfers between devices, fetch_weights(): lax.all_gather(edge_mat.astype(jnp.bfloat16), 'fsdp', axis=0, tiled=True)  48.7 us
    psum x1, blocking collectives, shards(): lax.psum((grad_lbias, grad_tbias, loss_sum), ('fsdp', 'rep'))  40.9 us
  transfers between devices with their start and end apart: 9, of which 8 were waited for; matrix products, arithmetic and copies ran while one was open for 13% of the time, Pallas kernels for 0%

commit v1 on v0

--- a/solution.py
+++ b/solution.py
@@ -200,7 +200,10 @@
             )
         else:
             full_in, full_out = (
-                lax.all_gather(own_in, "fsdp", axis=0, tiled=True),
+                jnp.concatenate(
+                    lax.all_to_all(jnp.stack([own_in] * lax.axis_size("fsdp")), "fsdp", 0, 0),
+                    axis=0,
+                ),
                 lax.all_gather(own_out, "fsdp", axis=0, tiled=True),
             )
         gathered_in.append(full_in)

time: 1390 us -> 1540 us (1.11)
  matrix products: 306 us -> 423 us
  waiting for transfers between devices: 651 us -> 571 us
  other arithmetic: 171 us -> 232 us
  local copies, waits for them, and re-layouts: 128 us -> 160 us
    dot_general x159 -> x198, matrix products: 285 us -> 375 us  [mult(): return jnp.einsum(form, left, right, preferred_element_type=jnp.float32)]
    reduce_scatter x1, waiting for transfers between devices: 73.4 us -> 0.01 us  [shards(): lax.psum_scatter(grad_out_full, 'fsdp', scatter_dimension=1, tiled=True)]
    reduce_scatter x1, waiting for transfers between devices: 279 us -> 224 us  [shards(): lax.psum_scatter(grad_in_full, 'fsdp', scatter_dimension=1, tiled=True)]
    all_gather x2, waiting for transfers between devices: 58.8 us -> 108 us  [fetch_weights(): lax.all_gather(own_out, 'fsdp', axis=0, tiled=True)]
    convert_element_type x22 -> x40, other arithmetic: 13.7 us -> 46.7 us  [round_value(): values.astype(jnp.bfloat16)]
    sub x6 -> x12, matrix products: 21.3 us -> 47.2 us  [block(): weights_soft = low(jax.nn.softmax(scores, axis=-1))]
    unnamed x1187 -> x1329, local copies, waits for them, and re-layouts: 31.5 us -> 29.2 us
  transfers between devices with their start and end apart: 9 -> 11, of which waited for: 8 -> 7; matrix products, arithmetic and copies ran while one was open for 13% -> 50% of each run, Pallas kernels for 0% -> 0%
where the time goes in v1:
time: 1540 us; the launch traced here: 1530 us
  waiting for transfers between devices  571 us (37%)
  matrix products  423 us (27%)
  other arithmetic  232 us (15%)
  local copies, waits for them, and re-layouts  160 us (10%)
  blocking collectives  99.7 us (6%)
  between operations  28.7 us (2%)
    dot_general x198, matrix products, mult(): return jnp.einsum(form, left, right, preferred_element_type=jnp.float32)  375 us
    reduce_scatter x1, waiting for transfers between devices, shards(): lax.psum_scatter(grad_in_full, 'fsdp', scatter_dimension=1, tiled=True)  224 us
    all_gather x2, waiting for transfers between devices, fetch_weights(): lax.all_gather(own_in, 'fsdp', axis=0, tiled=True)  119 us
    all_gather x2, waiting for transfers between devices, fetch_weights(): lax.all_gather(own_out, 'fsdp', axis=0, tiled=True)  108 us
    psum x1, waiting for transfers between devices, shards(): lax.psum((shard_in, shard_out, shard_edge), 'rep')  69.9 us
    all_gather x1, waiting for transfers between devices, fetch_weights(): lax.all_gather(edge_mat.astype(jnp.bfloat16), 'fsdp', axis=0, tiled=True)  49.2 us
    sub x12, matrix products, block(): weights_soft = low(jax.nn.softmax(scores, axis=-1))  47.2 us
    convert_element_type x40, other arithmetic, round_value(): values.astype(jnp.bfloat16)  46.7 us
  transfers between devices with their start and end apart: 11, of which 7 were waited for; matrix products, arithmetic and copies ran while one was open for 50% of the time, Pallas kernels for 0%

profile of v1, /device:TPU:0, one launch (start us, length us, event | category | flops | bytes accessed | tf_op | source)
XLA Modules:
  0.0 1527.9 jit_solution(3519152667923893285)
XLA Ops:
  16.4 7.5 all-to-all-start
  46.4 63.9 %all-gather.12.cloned.1.call-done = bf16[1,1536,384]{2,1,0:T(8,128)(2,1)} async-done(((bf16[1,192,384]{2,1,0:T(8,128)(2,1)}), bf16[1,1536,384]{2,1,0:T(8,128)(2,1)}) %all-gather.12.cloned.1.call-update) | async-done | bytes 1179664 | tf_op jit(solution)/shard_map/all_gather | solution.py:207
  110.3 43.6 %all-gather.14.cloned.1.call-done = bf16[1,1536,384]{2,1,0:T(8,128)(2,1)} async-done(((bf16[1,192,384]{2,1,0:T(8,128)(2,1)}), bf16[1,1536,384]{2,1,0:T(8,128)(2,1)}) %all-gather.14.cloned.1.call-update) | async-done | bytes 1179664 | tf_op jit(solution)/shard_map/all_gather | solution.py:207
  153.9 49.2 %all-gather.10.cloned.1.call-done = bf16[384,2457]{1,0:T(8,128)(2,1)} async-done(((bf16[48,2457]{1,0:T(8,128)(2,1)}), bf16[384,2457]{1,0:T(8,128)(2,1)}) %all-gather.10.cloned.1.call-update) | async-done | bytes 1886992 | tf_op jit(solution)/shard_map/all_gather | solution.py:214
  226.6 49.8 %all-gather.16.cloned.1.call-done = bf16[1,384,5376]{2,1,0:T(8,128)(2,1)} async-done(((bf16[1,48,5376]{2,1,0:T(8,128)(2,1)}), bf16[1,384,5376]{2,1,0:T(8,128)(2,1)}) %all-gather.16.cloned.1.call-update) | async-done | bytes 4128784 | tf_op jit(solution)/shard_map/all_gather | solution.py:198
  280.7 68.9 %all-gather.18.cloned.1.call-done = bf16[1,384,5376]{2,1,0:T(8,128)(2,1)} async-done(((bf16[1,48,5376]{2,1,0:T(8,128)(2,1)}), bf16[1,384,5376]{2,1,0:T(8,128)(2,1)}) %all-gather.18.cloned.1.call-update) | async-done | bytes 4128784 | tf_op jit(solution)/shard_map/all_gather | solution.py:198
  364.1 3.9 fusion.559
  376.7 5.0 multiply_convert_fusion.3
  389.5 4.0 fusion.560
  402.3 4.6 multiply_convert_fusion.2
  415.8 4.0 fusion.565
  429.0 4.7 multiply_convert_fusion.7
  444.9 4.6 fusion.566
  460.4 4.6 multiply_convert_fusion.6
  477.5 4.7 fusion.562
  493.1 4.6 multiply_convert_fusion.11
  509.1 4.6 fusion.563
  727.3 4.7 all-to-all-start.1
  776.5 3.9 multiply_reduce_fusion.21
  831.8 6.9 add_bitcast_fusion.6
  838.8 9.1 copy.871
  915.8 5.1 add_bitcast_fusion
  920.9 12.9 add_bitcast_fusion.4
  934.6 11.5 add_bitcast_fusion.1
  946.1 21.0 %add_add_fusion = f32[2,384,5376]{2,1,0:T(8,128)} fusion(f32[1,384,5376]{2,1,0:T(8,128)} %add_bitcast_fusion, f32[1,384,5376]{2,1,0:T(8,128)} %get-tuple-element.548, f32[1,384,5376]{2,1,0:T(8,128)S(1)} %add_bitcast_fusion.2, f32[1,384,5376]{2,1,0:T(8,128)} %get-tuple-element.549, f32[1,384,5376]{2,1,0:T(8,128)} %get-tuple-element.550, ...), kind=kLoop, calls=%fused_computation.21 | loop fusion | flops 20643840 | bytes 66060288 | tf_op jit(solution)/shard_map/add | solution.py:260
  986.4 4.0 fusion.113
  1080.2 4.1 fusion.570
  1104.6 44.3 %all-reduce.176 = (f32[]{:T(128)}, f32[2,5376]{1,0:T(2,128)S(1)}, f32[1952]{0:T(1024)S(1)}) all-reduce(f32[]{:T(128)S(6)} %add.2146, f32[2,5376]{1,0:T(2,128)S(1)} %add_add_fusion.26, f32[1952]{0:T(1024)S(1)} %add_add_fusion.27), channel_id=1, replica_groups=mesh['fsdp'=8,'rep'=4] {'fsdp','rep'}, use_global_device_ids=true, to_apply=%region_50.52 | all-reduce | flops 12705 | bytes 101640 | tf_op jit(solution)/shard_map/psum | solution.py:285
  1153.6 224.1 %reduce-scatter.3.cloned.1.call-done = f32[2,48,5376]{2,1,0:T(8,128)} async-done(((f32[2,384,5376]{2,1,0:T(8,128)}), f32[2,48,5376]{2,1,0:T(8,128)}) %reduce-scatter.3.cloned.1.call-update) | async-done | bytes 2064400 | tf_op jit(solution)/shard_map/reduce_scatter | solution.py:280
  1378.5 69.9 %all-reduce.185.cloned.1.call-done = (f32[2,48,5376]{2,1,0:T(8,128)}, f32[2,192,384]{2,1,0:T(8,128)}, f32[1,48,2457]{2,1,0:T(8,128)}) async-done(((f32[2,48,5376]{2,1,0:T(8,128)}, f32[2,192,384]{2,1,0:T(8,128)}, f32[1,48,2457]{2,1,0:T(8,128)}), (f32[2,48,5376]{2,1,0:T(8,128)}, f32[2,192,384]{2,1,0:T(8,128)}, f32[1,48,2457]{2,1,0:T(8,128)})) %all-reduce.185.cloned.1.call-update) | async-done | bytes 3125968 | tf_op jit(solution)/shard_map/psum | solution.py:284
  1454.3 37.6 %all-reduce.178 = (f32[2]{0:T(128)S(1)}, f32[2,5376]{1,0:T(2,128)S(1)}, f32[2]{0:T(128)S(1)}, f32[2,384]{1,0:T(2,128)S(1)}, f32[1]{0:T(128)}, /*index=5*/f32[1,2457]{1,0:T(1,128)S(1)}) all-reduce(f32[2]{0:T(128)S(1)} %get-tuple-element.165, f32[2,5376]{1,0:T(2,128)S(1)} %get-tuple-element.73, ...), channel_id=1, replica_groups=mesh['fsdp'=8,'rep'=4] {'fsdp'}, use_global_device_ids=true, to_apply=%region_159.162 | all-reduce | flops 13982 | bytes 111856 | tf_op jit(solution)/shard_map/psum | solution.py:304
  1494.5 17.8 %all-reduce.177 = (f32[2]{0:T(128)S(1)}, f32[2]{0:T(128)S(1)}, f32[1]{0:T(128)}) all-reduce(f32[2]{0:T(128)S(1)} %multiply_reduce_fusion.18, f32[2]{0:T(128)S(1)} %multiply_reduce_fusion.88, f32[1]{0:T(128)} %bitcast.216), channel_id=1, replica_groups=mesh['fsdp'=8,'rep'=4] {'fsdp'}, use_global_device_ids=true, to_apply=%region_161.164 | all-reduce | flops 5 | bytes 40 | tf_op jit(solution)/shard_map/psum | solution.py:321
  (2035 shorter events, 690.0 us)
Async XLA Ops:
  7.2 103.1 %all-gather.12.cloned.1.call-start = ((), (), s32[]{:S(2)}) async-start(), calls=%async_computation.7 | async-start | bytes 1327104 | tf_op jit(solution)/shard_map/all_gather | solution.py:207
  9.2 144.7 %all-gather.14.cloned.1.call-start = ((), (), s32[]{:S(2)}) async-start(), calls=%async_computation.8 | async-start | bytes 1327104 | tf_op jit(solution)/shard_map/all_gather | solution.py:207
  10.0 193.2 %all-gather.10.cloned.1.call-start = ((), (), s32[]{:S(2)}) async-start(), calls=%async_computation.4 | async-start | bytes 2211840 | tf_op jit(solution)/shard_map/all_gather | solution.py:214
  11.8 264.6 %all-gather.16.cloned.1.call-start = ((), (), s32[]{:S(2)}) async-start(), calls=%async_computation.9 | async-start | bytes 4644864 | tf_op jit(solution)/shard_map/all_gather | solution.py:198
  16.4 708.7 %all-to-all-start = ((bf16[8,48,5376]{2,1,0:T(8,128)(2,1)}), bf16[8,48,5376]{2,1,0:T(8,128)(2,1)}, u32[]{:S(2)}, u32[]{:S(2)}) async-start(bf16[8,48,5376]{2,1,0:T(8,128)(2,1)} %stack.9), calls=%async_computation | async-start | bytes 8257536 | tf_op jit(solution)/shard_map/all_to_all | solution.py:204
  23.8 325.8 %all-gather.18.cloned.1.call-start = ((), (), s32[]{:S(2)}) async-start(), calls=%async_computation.10 | async-start | bytes 4644864 | tf_op jit(solution)/shard_map/all_gather | solution.py:198
  29.0 175.3 %copy-start.619 = (bf16[2,256]{1,0:T(2,128)(2,1)}, bf16[2,256]{1,0:T(2,128)(2,1)S(1)}, u32[]{:S(2)}) copy-start(bf16[2,256]{1,0:T(2,128)(2,1)S(1)} %pad_maximum_fusion.5) | copy-start | bytes 3076
  31.9 177.3 %copy-start.621 = (bf16[2,256]{1,0:T(2,128)(2,1)}, bf16[2,256]{1,0:T(2,128)(2,1)S(1)}, u32[]{:S(2)}) copy-start(bf16[2,256]{1,0:T(2,128)(2,1)S(1)} %pad_maximum_fusion.4) | copy-start | bytes 3076
  34.2 179.3 %copy-start.623 = (bf16[2,256]{1,0:T(2,128)(2,1)}, bf16[2,256]{1,0:T(2,128)(2,1)S(1)}, u32[]{:S(2)}) copy-start(bf16[2,256]{1,0:T(2,128)(2,1)S(1)} %pad_maximum_fusion.3) | copy-start | bytes 3076
  42.7 356.4 %copy-start.294 = (f32[384]{0:T(512)}, f32[384]{0:T(512)S(1)}, u32[]{:S(2)}) copy-start(f32[384]{0:T(512)S(1)} %get-tuple-element.125) | copy-start | bytes 4612
  43.9 310.5 %copy-start.230 = (f32[2304]{0:T(1024)}, f32[2304]{0:T(1024)S(1)}, u32[]{:S(2)}) copy-start(f32[2304]{0:T(1024)S(1)} %get-tuple-element.135) | copy-start | bytes 27652
  44.0 312.9 %copy-start.228 = (f32[2304]{0:T(1024)}, f32[2304]{0:T(1024)S(1)}, u32[]{:S(2)}) copy-start(f32[2304]{0:T(1024)S(1)} %get-tuple-element.134) | copy-start | bytes 27652
  45.8 160.4 %copy-start.641 = (f32[384]{0:T(512)}, f32[384]{0:T(512)S(1)}, u32[]{:S(2)}) copy-start(f32[384]{0:T(512)S(1)} %get-tuple-element.358) | copy-start | bytes 4612
  209.2 140.3 %copy-start.312 = (bf16[2,384]{1,0:T(2,128)(2,1)}, bf16[2,384]{1,0:T(2,128)(2,1)S(1)}, u32[]{:S(2)}) copy-start(bf16[2,384]{1,0:T(2,128)(2,1)S(1)} %get-tuple-element.223) | copy-start | bytes 4612
  213.5 138.5 %copy-start.315 = (bf16[2,384]{1,0:T(2,128)(2,1)}, bf16[2,384]{1,0:T(2,128)(2,1)S(1)}, u32[]{:S(2)}) copy-start(bf16[2,384]{1,0:T(2,128)(2,1)S(1)} %get-tuple-element.219) | copy-start | bytes 4612
  217.9 139.0 %copy-start.319 = (bf16[2,384]{1,0:T(2,128)(2,1)}, bf16[2,384]{1,0:T(2,128)(2,1)S(1)}, u32[]{:S(2)}) copy-start(bf16[2,384]{1,0:T(2,128)(2,1)S(1)} %get-tuple-element.215) | copy-start | bytes 4612
  219.3 154.3 %copy-start = (f32[2,256,384]{2,1,0:T(8,128)}, f32[2,256,384]{2,1,0:T(8,128)S(1)}, u32[]{:S(2)}) copy-start(f32[2,256,384]{2,1,0:T(8,128)S(1)} %get-tuple-element.411) | copy-start | bytes 2359300
  219.4 140.6 %copy-start.375 = (f32[2,256]{1,0:T(2,128)}, f32[2,256]{1,0:T(2,128)S(1)}, u32[]{:S(2)}) copy-start(f32[2,256]{1,0:T(2,128)S(1)} %broadcast_multiply_fusion.17) | copy-start | bytes 6148
  221.0 204.3 %copy-start.3 = (f32[2,256,384]{2,1,0:T(8,128)}, f32[2,256,384]{2,1,0:T(8,128)S(1)}, u32[]{:S(2)}) copy-start(f32[2,256,384]{2,1,0:T(8,128)S(1)} %get-tuple-element.444) | copy-start | bytes 2359300
  222.6 129.4 %copy-start.496 = (f32[2,256]{1,0:T(2,128)}, f32[2,256]{1,0:T(2,128)S(1)}, u32[]{:S(2)}) copy-start(f32[2,256]{1,0:T(2,128)S(1)} %multiply_reduce_fusion.87) | copy-start | bytes 6148
  222.7 137.3 %copy-start.467 = (f32[2,256]{1,0:T(2,128)}, f32[2,256]{1,0:T(2,128)S(1)}, u32[]{:S(2)}) copy-start(f32[2,256]{1,0:T(2,128)S(1)} %fusion.437) | copy-start | bytes 6148
  727.3 263.1 %all-to-all-start.1 = ((bf16[8,48,5376]{2,1,0:T(8,128)(2,1)}), bf16[8,48,5376]{2,1,0:T(8,128)(2,1)}, u32[]{:S(2)}, u32[]{:S(2)}) async-start(bf16[8,48,5376]{2,1,0:T(8,128)(2,1)} %stack.11), calls=%async_computation.1 | async-start | bytes 8257536 | tf_op jit(solution)/shard_map/all_to_all | solution.py:204
  732.1 419.7 %all-reduce.183.cloned.1.call-start = ((), (), s32[]{:S(2)}) async-start(), calls=%async_computation.11 | async-start | bytes 7864320
  847.9 305.7 %reduce-scatter.5.cloned.1.call-start = ((), (), s32[]{:S(2)}) async-start(), calls=%async_computation.6 | async-start | bytes 5308416 | tf_op jit(solution)/shard_map/reduce_scatter | solution.py:281
  876.9 500.8 %reduce-scatter.3.cloned.1.call-start = ((), (), s32[]{:S(2)}) async-start(), calls=%async_computation.5 | async-start | bytes 18579456 | tf_op jit(solution)/shard_map/reduce_scatter | solution.py:280
  967.2 481.2 %all-reduce.185.cloned.1.call-start = ((), (), s32[]{:S(2)}) async-start(), calls=%async_computation.12 | async-start | bytes 6291456 | tf_op jit(solution)/shard_map/psum | solution.py:284
  1103.5 274.2 %copy-start.267 = (f32[2,5376]{1,0:T(2,128)S(1)}, f32[2,5376]{1,0:T(2,128)}, u32[]{:S(2)}) copy-start(f32[2,5376]{1,0:T(2,128)} %param.28) | copy-start | bytes 129028
  1149.6 301.3 %copy-start.466 = (f32[1952]{0:T(1024)}, f32[1952]{0:T(1024)S(1)}, u32[]{:S(2)}) copy-start(f32[1952]{0:T(1024)S(1)} %get-tuple-element.158) | copy-start | bytes 23428
  1151.7 299.2 %copy-start.268 = (f32[2,5376]{1,0:T(2,128)}, f32[2,5376]{1,0:T(2,128)S(1)}, u32[]{:S(2)}) copy-start(f32[2,5376]{1,0:T(2,128)S(1)} %get-tuple-element.160) | copy-start | bytes 129028
  1377.7 114.2 %copy-start.392 = (f32[2457]{0:T(1024)S(1)}, f32[2457]{0:T(1024)}, u32[]{:S(2)}) copy-start(f32[2457]{0:T(1024)} %broadcast_multiply_fusion) | copy-start | bytes 29488
  1377.7 114.9 %copy-start.630 = (f32[2,384]{1,0:T(2,128)S(1)}, f32[2,384]{1,0:T(2,128)}, u32[]{:S(2)}) copy-start(f32[2,384]{1,0:T(2,128)} %param.33) | copy-start | bytes 9220
  1377.7 114.9 %copy-start.441 = (f32[2,5376]{1,0:T(2,128)S(1)}, f32[2,5376]{1,0:T(2,128)}, u32[]{:S(2)}) copy-start(f32[2,5376]{1,0:T(2,128)} %param.31) | copy-start | bytes 129028
  (645 other events, 3707.6 us)
Sparse Core Ops, SparseCore 0:
  10.2 100.0 all-gather.11
  112.5 41.4 all-gather.13
  156.7 46.4 all-gather.9
  205.8 70.5 all-gather.15
  279.0 70.4 all-gather.17
  848.0 150.7 all-reduce.182
  1002.5 94.6 reduce-scatter.4
  1101.2 276.4 reduce-scatter.2
  1380.8 67.5 all-reduce.184
